TPU v7x, 128 devices: a whole 4x4x4 slice. The times are simulated.
128 devices in a mesh: freq: 8 (over x, z_hi), panel: 16 (over z_lo, y, core).
Axes of the slice: x: 4, y: 4, z: 4 (z_hi: 2, z_lo: 2; z = z_hi * 2 + z_lo), core: 2. Of those that a mesh axis runs over, the one named last changes fastest.
Arguments:
- traces: bfloat16 [640, 640, 1024], P('panel', 'freq'), may hold values from -6 to 6
- filters: float32 [16, 7, 64], replicated, may hold values from -0.25 to 0.25
Outputs:
- primaries: bfloat16 [640, 640, 1024], P('panel', 'freq')
All inputs are finite; a program needn't handle non-finite values.
Results may differ from a plain program's by a relative error of at most 0.0095.
Values may be sent and summed in bfloat16 or wider, within the bound.
No kernel may reach another device: no remote copies, remote signals or barrier semaphores. Data moves between devices by JAX's collectives and lax.ppermute only.
A program may use at most 128 MiB of HBM per device.

v0:
```python
import math
import jax
import jax.numpy as jnp
from jax import lax
from jax.sharding import PartitionSpec as P

NS = 640
NT = 1024
NF = 96
FLO = 8
TAPS = 64
SPAN = 7
RWIN = 40


def wave_table(freq_bins, sample_index):
    phases = freq_bins[:, None] * sample_index[None, :] % NT
    angles = phases.astype(jnp.float32) * jnp.float32(2.0 * math.pi / NT)
    return (jnp.cos(angles), jnp.sin(angles))


def complex_product(left_side, right_side):

    def factor_product(leading_factor, trailing_factor):
        return jnp.einsum(
            "gjo,god->gjd", leading_factor, trailing_factor, preferred_element_type=jnp.float32
        )

    part_real = factor_product(left_side[0], right_side[0]) - factor_product(
        left_side[1], right_side[1]
    )
    part_imag = factor_product(left_side[0], right_side[1]) + factor_product(
        left_side[1], right_side[0]
    )
    return jnp.stack([part_real, part_imag])


def response(filters, freq_bins):
    tap_index = jnp.arange(TAPS, dtype=jnp.int32)
    cosine_wave, sine_wave = wave_table(freq_bins, tap_index)
    filter_real = jnp.einsum("fk,wjk->fjw", cosine_wave, filters)
    filter_imag = -jnp.einsum("fk,wjk->fjw", sine_wave, filters)
    return (jnp.repeat(filter_real, RWIN, axis=2), jnp.repeat(filter_imag, RWIN, axis=2))


def apply_filter(extended, filter_real, filter_imag, source_count):
    sum_real = jnp.zeros(extended.shape[1:2] + (source_count,) + extended.shape[3:], jnp.float32)
    sum_imag = jnp.zeros_like(sum_real)
    for shifted in range(SPAN):
        part_real = extended[0, :, shifted : shifted + source_count, :]
        part_imag = extended[1, :, shifted : shifted + source_count, :]
        weight_real = filter_real[:, shifted][:, None, :]
        weight_imaginary = filter_imag[:, shifted][:, None, :]
        sum_real = sum_real + weight_real * part_real - weight_imaginary * part_imag
        sum_imag = sum_imag + weight_real * part_imag + weight_imaginary * part_real
    return jnp.stack([sum_real, sum_imag])


def per_device(traces, filters):
    shot_rows, receiver_cols, time_sample_count = traces.shape
    rim_width = SPAN // 2
    scale_sources = jnp.float32(math.sqrt(NS))
    freq_bins = FLO + jnp.arange(NF, dtype=jnp.int32)
    cosine_wave, sine_wave = wave_table(freq_bins, jnp.arange(NT, dtype=jnp.int32))
    forward = (jnp.concatenate([cosine_wave, -sine_wave], 0) / jnp.float32(math.sqrt(NT))).astype(
        jnp.bfloat16
    )
    reciprocal_value = jnp.concatenate([cosine_wave, -sine_wave], 0).astype(jnp.bfloat16)
    spectra = jnp.einsum("srt,ct->csr", traces, forward, preferred_element_type=jnp.float32)
    spectra = spectra.astype(jnp.bfloat16).reshape(2, NF, shot_rows, receiver_cols)
    columns = lax.all_to_all(spectra, "panel", split_axis=1, concat_axis=2, tiled=True)
    slice_count = columns.shape[1]
    first_slice = lax.axis_index("panel") * slice_count
    complete = lax.all_gather(columns, "freq", axis=3, tiled=True)
    order_one = (complex_product(complete, columns) / scale_sources).astype(jnp.bfloat16)
    order_two = complex_product(complete, order_one) / scale_sources
    prediction = (order_one.astype(jnp.float32) - order_two).astype(jnp.bfloat16)
    extended = jnp.pad(
        prediction.astype(jnp.float32), ((0, 0), (0, 0), (rim_width, rim_width), (0, 0))
    )
    own_bins = FLO + first_slice + jnp.arange(slice_count, dtype=jnp.int32)
    filter_real, filter_imag = response(filters, own_bins)
    receiver_start = lax.axis_index("freq") * receiver_cols
    filter_real = lax.dynamic_slice_in_dim(filter_real, receiver_start, receiver_cols, 2)
    filter_imag = lax.dynamic_slice_in_dim(filter_imag, receiver_start, receiver_cols, 2)
    matched = apply_filter(extended, filter_real, filter_imag, NS)
    returned = lax.all_to_all(
        matched.astype(jnp.bfloat16), "panel", split_axis=2, concat_axis=1, tiled=True
    )
    matched_rows = returned.reshape(2 * NF, shot_rows, receiver_cols)
    multiples = jnp.einsum(
        "csr,ct->srt", matched_rows, reciprocal_value, preferred_element_type=jnp.float32
    )
    multiples = multiples / jnp.float32(math.sqrt(NF))
    return (traces.astype(jnp.float32) - multiples).astype(jnp.bfloat16)


def solution(mesh):
    placed = (P("panel", "freq", None), P())
    return jax.shard_map(
        per_device, mesh=mesh, in_specs=placed, out_specs=P("panel", "freq", None), check_vma=False
    )
```

profile of v0, /device:TPU:1, one launch (start us, length us, event | category | flops | bytes accessed | tf_op | source)
XLA Modules:
  0.0 312.2 jit_solution(14349941599640643925)
XLA Ops:
  6.5 1.6 fusion.58
  9.1 4.8 %convolution_convert_fusion = bf16[192,40,80]{0,2,1:T(8,128)(2,1)S(1)} fusion(bf16[40,80,1024]{2,1,0:T(8,128)(2,1)} %param.2, f32[96,1024]{1,0:T(8,128)S(1)} %get-tuple-element.24, f32[96,1024]{1,0:T(8,128)S(1)} %get-tuple-element.23), kind=kOutput, calls=%fused_computation.35 | convolution fusion | flops 1259495424 | bytes 8568832 | tf_op jit(solution)/shard_map/srt,ct->csr/dot_general | solution.py:69
  14.7 3.3 %copy.54 = bf16[2,96,40,80]{3,2,0,1:T(8,128)(2,1)} copy(bf16[2,96,40,80]{1,0,3,2:T(2,128)(2,1)S(1)} %reshape.26) | data formatting | bytes 2457600 | tf_op jit(solution)/shard_map/reshape | solution.py:70
  18.1 32.3 %all_to_all.33 = bf16[2,96,40,80]{3,2,0,1:T(8,128)(2,1)S(1)} all-to-all(bf16[2,96,40,80]{3,2,0,1:T(8,128)(2,1)} %copy.54), channel_id=1, replica_groups=mesh['freq'=8,'panel'=16] {'panel'}, dimensions={1} | all-to-all | bytes 2457600 | tf_op jit(solution)/shard_map/all_to_all | solution.py:71
  50.4 1.7 copy.56
  52.2 4.5 %copy.57 = bf16[2,6,640,80]{2,0,1,3:T(2,128)(2,1)} copy(bf16[2,6,640,80]{3,2,1,0:T(8,128)(2,1)} %bitcast.140) | data formatting | bytes 2457600 | tf_op jit(solution)/shard_map/all_to_all | solution.py:71
  59.3 118.6 %all-gather.2.cloned.1.call-done = bf16[2,6,640,640]{2,0,1,3:T(2,128)(2,1)} async-done(((bf16[2,6,640,80]{2,0,1,3:T(2,128)(2,1)}), bf16[2,6,640,640]{2,0,1,3:T(2,128)(2,1)}) %all-gather.2.cloned.1.call-update) | async-done | bytes 9830416 | tf_op jit(solution)/shard_map/all_gather | solution.py:74
  177.9 20.6 %fusion.80 = (bf16[1,6,640,640]{2,0,1,3:T(2,128)(2,1)}, bf16[1,6,640,640]{2,0,1,3:T(2,128)(2,1)}) fusion(bf16[2,6,640,640]{2,0,1,3:T(2,128)(2,1)} %all-gather.2.cloned.1.call-done), kind=kLoop, calls=%fused_computation.122 | loop fusion | bytes 19660800 | tf_op jit(solution)/shard_map/slice | solution.py:29
  198.5 19.7 %copy.91 = bf16[1,6,640,640]{3,2,1,0:T(8,128)(2,1)} copy(bf16[1,6,640,640]{2,0,1,3:T(2,128)(2,1)} %get-tuple-element.6) | data formatting | bytes 9830400
  218.3 19.8 %copy.90 = bf16[1,6,640,640]{3,2,1,0:T(8,128)(2,1)} copy(bf16[1,6,640,640]{2,0,1,3:T(2,128)(2,1)} %get-tuple-element.5) | data formatting | bytes 9830400
  238.0 4.2 %fusion.6 = f32[6,640,80]{1,2,0:T(8,128)S(1)} fusion(bf16[6,640,80]{2,1,0:T(8,128)(2,1)S(1)} %bitcast.133, bf16[1,6,640,640]{3,2,1,0:T(8,128)(2,1)} %copy.91), kind=kOutput, calls=%fused_computation.7 | convolution fusion | flops 393216000 | bytes 6758400 | tf_op jit(solution)/shard_map/gjo,god->gjd/dot_general | solution.py:25
  242.2 1.7 fusion.4
  244.6 1.7 fusion.23
  246.3 1.7 fusion.29
  248.2 1.7 fusion.2
  249.8 1.7 fusion
  251.5 1.7 fusion.35
  253.2 1.7 fusion.41
  255.2 5.4 %subtract_convert_fusion.1 = bf16[1,6,640,80]{2,3,1,0:T(8,128)(2,1)S(1)} fusion(f32[2,6,640,80]{2,3,1,0:T(8,128)S(1)} %fusion.44, f32[6,80]{1,0:T(8,128)S(1)} %bitcast.143, f32[6,80]{1,0:T(8,128)S(1)} %bitcast.145, f32[6,80]{1,0:T(8,128)S(1)} %bitcast.147, f32[6,80]{1,0:T(8,128)S(1)} %bitcast.149, f32[6,80]{1,0:T(8,128)S(1)} %bitcast.151, ...), kind=kLoop, calls=%fused_computation.47 | loop fusion | flops 8601600 | bytes 5586944 | tf_op jit(solution)/shard_map/convert
  260.6 5.3 %add_convert_fusion = bf16[1,6,640,80]{2,3,1,0:T(8,128)(2,1)S(1)} fusion(f32[2,6,640,80]{2,3,1,0:T(8,128)S(1)} %fusion.44, f32[6,80]{1,0:T(8,128)S(1)} %bitcast.144, f32[6,80]{1,0:T(8,128)S(1)} %bitcast.146, f32[6,80]{1,0:T(8,128)S(1)} %bitcast.148, f32[6,80]{1,0:T(8,128)S(1)} %bitcast.150, f32[6,80]{1,0:T(8,128)S(1)} %bitcast.152, ...), kind=kLoop, calls=%fused_computation.46 | loop fusion | flops 8601600 | bytes 5586944 | tf_op jit(solution)/shard_map/convert.1
  266.1 2.6 copy.67
  268.7 30.9 %all_to_all.34 = bf16[2,6,640,80]{3,0,1,2:T(2,128)(2,1)S(1)} all-to-all(bf16[2,6,640,80]{3,0,1,2:T(2,128)(2,1)S(1)} %copy.67), channel_id=1, replica_groups=mesh['freq'=8,'panel'=16] {'panel'}, dimensions={2} | all-to-all | bytes 2457600 | tf_op jit(solution)/shard_map/all_to_all | solution.py:87
  300.3 0.9 slice-done.1
  301.4 4.0 %subtract_convert_fusion = bf16[40,80,1024]{2,1,0:T(8,128)(2,1)} fusion(bf16[40,80,1024]{2,1,0:T(8,128)(2,1)S(1)} %bitcast.142, bf16[192,40,80]{2,1,0:T(8,128)(2,1)S(1)} %bitcast.138, f32[96,1024]{1,0:T(8,128)S(1)} %copy-done.7, f32[96,1024]{1,0:T(8,128)S(1)} %copy-done.5), kind=kOutput, calls=%fused_computation | convolution fusion | flops 1272184832 | bytes 15122432 | tf_op jit(solution)/shard_map/csr,ct->srt/dot_general | solution.py:91
  (57 shorter events, 6.6 us)
Async XLA Ops:
  6.5 50.2 %copy-start = (f32[16,7,64]{2,0,1:T(8,128)S(1)}, f32[16,7,64]{2,0,1:T(8,128)}, u32[]{:S(2)}) copy-start(f32[16,7,64]{2,0,1:T(8,128)} %param.3) | copy-start | bytes 86020
  6.5 171.3 %all-gather.2.cloned.1.call-start = ((), (), s32[]{:S(2)}) async-start(), calls=%async_computation.2 | async-start | bytes 11059200 | tf_op jit(solution)/shard_map/all_gather | solution.py:74
  8.2 0.8 copy-start.4
  8.2 0.9 copy-start.6
  238.0 4.2 %copy-start.2 = (bf16[1,6,640,640]{3,2,1,0:T(8,128)(2,1)S(1)}, bf16[1,6,640,640]{3,2,1,0:T(8,128)(2,1)}, u32[]{:S(2)}) copy-start(bf16[1,6,640,640]{3,2,1,0:T(8,128)(2,1)} %copy.91) | copy-start | bytes 14745604
  242.2 2.4 copy-start.3
  268.6 31.6 %slice-start = ((s8[6553600]{0:T(1024)(128)(4,1)}), s8[4194304]{0:T(1024)(128)(4,1)S(1)}, s32[]{:S(2)}) async-start(s8[6553600]{0:T(1024)(128)(4,1)} %bitcast.141), calls=%async_computation.3 | async-start | bytes 8388608
  299.5 1.7 slice-start.1
  299.9 1.4 copy-start.5
  299.9 1.5 copy-start.7
  301.4 4.0 %copy-start.1 = (f32[16,7,64]{2,0,1:T(8,128)S(1)}, f32[16,7,64]{2,0,1:T(8,128)}, u32[]{:S(2)}) copy-start(f32[16,7,64]{2,0,1:T(8,128)} %param.3) | copy-start | bytes 86020
Sparse Core Ops, SparseCore 0:
  56.8 120.9 all-gather.1
where the time goes:
time: 314 us; the launch traced here: 312 us
  waiting for transfers between devices  119 us (38%)
  local copies, waits for them, and re-layouts  78.6 us (25%)
  blocking collectives  63.2 us (20%)
  matrix products  25 us (8%)
  between operations  13.7 us (4%)
  other arithmetic  13.1 us (4%)
    all_gather x1, waiting for transfers between devices, per_device(): complete = lax.all_gather(columns, 'freq', axis=3, tiled=True)  119 us
    unnamed x36, local copies, waits for them, and re-layouts  42.4 us
    all_to_all x1, blocking collectives, per_device(): lax.all_to_all(spectra, 'panel', split_axis=1, concat_axis=2, tiled=True)  32.3 us
    all_to_all x1, blocking collectives, per_device(): lax.all_to_all(matched.astype(jnp.bfloat16), 'panel', split_axis=2, conca...  30.9 us
    slice x1, local copies, waits for them, and re-layouts, complex_product(): left_side[0]  20.6 us
    dot_general x8, matrix products, factor_product(): jnp.einsum('gjo,god->gjd', leading_factor, trailing_factor, preferred_ele...  15.8 us
    another operation x2, other arithmetic  10.7 us
    all_to_all x3, local copies, waits for them, and re-layouts, per_device(): lax.all_to_all(spectra, 'panel', split_axis=1, concat_axis=2, tiled=True)  6.6 us
  transfers between devices with their start and end apart: 1, of which 1 were waited for; matrix products, arithmetic and copies ran while one was open for 1% of the time, Pallas kernels for 0%

commit v1 on v0

--- a/solution.py
+++ b/solution.py
@@ -84,8 +84,14 @@
     filter_real = lax.dynamic_slice_in_dim(filter_real, receiver_start, receiver_cols, 2)
     filter_imag = lax.dynamic_slice_in_dim(filter_imag, receiver_start, receiver_cols, 2)
     matched = apply_filter(extended, filter_real, filter_imag, NS)
-    returned = lax.all_to_all(
-        matched.astype(jnp.bfloat16), "panel", split_axis=2, concat_axis=1, tiled=True
+    returned = jnp.concatenate(
+        lax.all_to_all(
+            jnp.stack(jnp.split(matched.astype(jnp.bfloat16), lax.axis_size("panel"), axis=2)),
+            "panel",
+            0,
+            0,
+        ),
+        axis=1,
     )
     matched_rows = returned.reshape(2 * NF, shot_rows, receiver_cols)
     multiples = jnp.einsum(

time: 314 us -> 329 us (1.048)
  other arithmetic: 13.1 us -> 26.5 us
    unnamed x1 -> x15, other arithmetic: 0.01 us -> 12.4 us
    unnamed x36 -> x32, local copies, waits for them, and re-layouts: 42.4 us -> 42 us
where the time goes in v1:
time: 329 us; the launch traced here: 327 us
  waiting for transfers between devices  119 us (36%)
  local copies, waits for them, and re-layouts  78.7 us (24%)
  blocking collectives  63 us (19%)
  matrix products  26.9 us (8%)
  other arithmetic  26.5 us (8%)
  between operations  13.7 us (4%)
    all_gather x1, waiting for transfers between devices, per_device(): complete = lax.all_gather(columns, 'freq', axis=3, tiled=True)  119 us
    unnamed x32, local copies, waits for them, and re-layouts  42 us
    all_to_all x1, blocking collectives, per_device(): lax.all_to_all(spectra, 'panel', split_axis=1, concat_axis=2, tiled=True)  32.3 us
    all_to_all x1, blocking collectives, per_device(): lax.all_to_all(jnp.stack(jnp.split(matched.astype(jnp.bfloat16), lax.axis...  30.6 us
    slice x1, local copies, waits for them, and re-layouts, complex_product(): left_side[0]  20.5 us
    dot_general x8, matrix products, factor_product(): jnp.einsum('gjo,god->gjd', leading_factor, trailing_factor, preferred_ele...  15.8 us
    unnamed x15, other arithmetic  12.4 us
    another operation x2, other arithmetic  10.9 us
  transfers between devices with their start and end apart: 1, of which 1 were waited for; matrix products, arithmetic and copies ran while one was open for 1% of the time, Pallas kernels for 0%

profile of v1, /device:TPU:1, one launch (start us, length us, event | category | flops | bytes accessed | tf_op | source)
XLA Modules:
  0.0 327.4 jit_solution(3103156317381301593)
XLA Ops:
  6.5 1.6 fusion.105
  9.1 4.8 %convolution_convert_fusion = bf16[192,40,80]{0,2,1:T(8,128)(2,1)S(1)} fusion(bf16[40,80,1024]{2,1,0:T(8,128)(2,1)} %param.2, f32[96,1024]{1,0:T(8,128)S(1)} %get-tuple-element.24, f32[96,1024]{1,0:T(8,128)S(1)} %get-tuple-element.23), kind=kOutput, calls=%fused_computation.65 | convolution fusion | flops 1259495424 | bytes 8568832 | tf_op jit(solution)/shard_map/srt,ct->csr/dot_general | solution.py:69
  13.9 0.9 reshape.25
  14.7 3.3 %copy.33 = bf16[2,96,40,80]{3,2,0,1:T(8,128)(2,1)} copy(bf16[2,96,40,80]{1,0,3,2:T(2,128)(2,1)S(1)} %reshape.25) | data formatting | bytes 2457600 | tf_op jit(solution)/shard_map/reshape | solution.py:70
  18.1 32.3 %all_to_all.23 = bf16[2,96,40,80]{3,2,0,1:T(8,128)(2,1)S(1)} all-to-all(bf16[2,96,40,80]{3,2,0,1:T(8,128)(2,1)} %copy.33), channel_id=1, replica_groups=mesh['freq'=8,'panel'=16] {'panel'}, dimensions={1} | all-to-all | bytes 2457600 | tf_op jit(solution)/shard_map/all_to_all | solution.py:71
  50.4 1.7 copy.35
  52.2 4.5 %copy.36 = bf16[2,6,640,80]{2,0,1,3:T(2,128)(2,1)} copy(bf16[2,6,640,80]{3,2,1,0:T(8,128)(2,1)} %bitcast.202) | data formatting | bytes 2457600 | tf_op jit(solution)/shard_map/all_to_all | solution.py:71
  59.3 118.6 %all-gather.2.cloned.1.call-done = bf16[2,6,640,640]{2,0,1,3:T(2,128)(2,1)} async-done(((bf16[2,6,640,80]{2,0,1,3:T(2,128)(2,1)}), bf16[2,6,640,640]{2,0,1,3:T(2,128)(2,1)}) %all-gather.2.cloned.1.call-update) | async-done | bytes 9830416 | tf_op jit(solution)/shard_map/all_gather | solution.py:74
  177.9 20.5 %fusion.127 = (bf16[1,6,640,640]{2,0,1,3:T(2,128)(2,1)}, bf16[1,6,640,640]{2,0,1,3:T(2,128)(2,1)}) fusion(bf16[2,6,640,640]{2,0,1,3:T(2,128)(2,1)} %all-gather.2.cloned.1.call-done), kind=kLoop, calls=%fused_computation.199 | loop fusion | bytes 19660800 | tf_op jit(solution)/shard_map/slice | solution.py:29
  198.4 19.7 %copy.69 = bf16[1,6,640,640]{3,2,1,0:T(8,128)(2,1)} copy(bf16[1,6,640,640]{2,0,1,3:T(2,128)(2,1)} %get-tuple-element.6) | data formatting | bytes 9830400
  218.1 19.7 %copy.68 = bf16[1,6,640,640]{3,2,1,0:T(8,128)(2,1)} copy(bf16[1,6,640,640]{2,0,1,3:T(2,128)(2,1)} %get-tuple-element.5) | data formatting | bytes 9830400
  237.9 4.2 %fusion.6 = f32[6,640,80]{1,2,0:T(8,128)S(1)} fusion(bf16[6,640,80]{2,1,0:T(8,128)(2,1)S(1)} %bitcast.195, bf16[1,6,640,640]{3,2,1,0:T(8,128)(2,1)} %copy.69), kind=kOutput, calls=%fused_computation.7 | convolution fusion | flops 393216000 | bytes 6758400 | tf_op jit(solution)/shard_map/gjo,god->gjd/dot_general | solution.py:25
  242.1 1.7 fusion.4
  244.5 1.7 fusion.23
  246.1 1.7 fusion.29
  248.0 1.7 fusion.2
  249.7 1.7 fusion
  251.3 1.7 fusion.35
  253.0 1.7 fusion.41
  255.2 5.3 %add_convert_fusion = bf16[1,6,640,80]{2,3,1,0:T(8,128)(2,1)S(1)} fusion(f32[2,6,640,80]{2,3,1,0:T(8,128)S(1)} %fusion.44, f32[6,80]{1,0:T(8,128)S(1)} %bitcast.203, f32[6,80]{1,0:T(8,128)S(1)} %bitcast.205, f32[6,80]{1,0:T(8,128)S(1)} %bitcast.207, f32[6,80]{1,0:T(8,128)S(1)} %bitcast.209, f32[6,80]{1,0:T(8,128)S(1)} %bitcast.211, ...), kind=kLoop, calls=%fused_computation.75 | loop fusion | flops 8601600 | bytes 5586944 | tf_op jit(solution)/shard_map/convert.1
  260.5 5.6 %subtract_convert_fusion.1 = bf16[1,6,640,80]{2,3,1,0:T(8,128)(2,1)S(1)} fusion(f32[2,6,640,80]{2,3,1,0:T(8,128)S(1)} %fusion.44, f32[6,80]{1,0:T(8,128)S(1)} %bitcast.204, f32[6,80]{1,0:T(8,128)S(1)} %bitcast.206, f32[6,80]{1,0:T(8,128)S(1)} %bitcast.208, f32[6,80]{1,0:T(8,128)S(1)} %bitcast.210, f32[6,80]{1,0:T(8,128)S(1)} %bitcast.212, ...), kind=kLoop, calls=%fused_computation.76 | loop fusion | flops 8601600 | bytes 5586944 | tf_op jit(solution)/shard_map/convert
  279.3 3.6 %copy.46 = bf16[16,2,6,40,80]{4,3,2,1,0:T(8,128)(2,1)S(1)} copy(bf16[16,2,6,40,80]{3,4,2,1,0:T(8,128)(2,1)} %fusion.104) | data formatting | bytes 2457600 | tf_op jit(solution)/shard_map/stack | solution.py:89
  282.9 30.6 %all_to_all.24 = bf16[16,2,6,40,80]{4,3,2,1,0:T(8,128)(2,1)S(1)} all-to-all(bf16[16,2,6,40,80]{4,3,2,1,0:T(8,128)(2,1)S(1)} %copy.46), channel_id=1, replica_groups=mesh['freq'=8,'panel'=16] {'panel'}, dimensions={0} | all-to-all | bytes 2457600 | tf_op jit(solution)/shard_map/all_to_all | solution.py:88
  314.6 5.9 %subtract_convert_fusion = bf16[40,80,1024]{2,1,0:T(8,128)(2,1)} fusion(bf16[40,80,1024]{2,1,0:T(8,128)(2,1)} %param.2, bf16[192,40,80]{2,1,0:T(8,128)(2,1)S(1)} %bitcast.200, f32[96,1024]{1,0:T(8,128)S(1)} %copy-done.7, f32[96,1024]{1,0:T(8,128)S(1)} %copy-done.5), kind=kOutput, calls=%fused_computation | convolution fusion | flops 1272184832 | bytes 15122432 | tf_op jit(solution)/shard_map/csr,ct->srt/dot_general | solution.py:97
  (66 shorter events, 19.1 us)
Async XLA Ops:
  6.5 50.2 %copy-start = (f32[16,7,64]{2,0,1:T(8,128)S(1)}, f32[16,7,64]{2,0,1:T(8,128)}, u32[]{:S(2)}) copy-start(f32[16,7,64]{2,0,1:T(8,128)} %param.3) | copy-start | bytes 86020
  6.5 171.3 %all-gather.2.cloned.1.call-start = ((), (), s32[]{:S(2)}) async-start(), calls=%async_computation.2 | async-start | bytes 11059200 | tf_op jit(solution)/shard_map/all_gather | solution.py:74
  8.2 0.8 copy-start.4
  8.2 0.9 copy-start.6
  237.9 4.2 %copy-start.2 = (bf16[1,6,640,640]{3,2,1,0:T(8,128)(2,1)S(1)}, bf16[1,6,640,640]{3,2,1,0:T(8,128)(2,1)}, u32[]{:S(2)}) copy-start(bf16[1,6,640,640]{3,2,1,0:T(8,128)(2,1)} %copy.69) | copy-start | bytes 14745604
  242.1 2.4 copy-start.3
  313.5 1.0 copy-start.5
  313.5 1.1 copy-start.7
  314.6 5.9 %copy-start.1 = (f32[16,7,64]{2,0,1:T(8,128)S(1)}, f32[16,7,64]{2,0,1:T(8,128)}, u32[]{:S(2)}) copy-start(f32[16,7,64]{2,0,1:T(8,128)} %param.3) | copy-start | bytes 86020
Sparse Core Ops, SparseCore 0:
  56.8 120.9 all-gather.1
